TPU v7x, 32 devices: a whole 2x2x4 slice. The times are simulated.
32 devices in a mesh: seq: 16 (over z, y, x), tp: 2 (over core).
Axes of the slice: x: 2, y: 2, z: 4, core: 2. Of those that a mesh axis runs over, the one named last changes fastest.
Arguments:
- img_qkv: bfloat16 [1, 512, 3, 2048], P(None, 'seq', None, 'tp'), may hold values from -7 to 7
- txt_qkv: bfloat16 [1, 256, 3, 2048], P(None, None, None, 'tp'), may hold values from -7 to 7
- frame_index: int32 [1, 512], P(None, 'seq'), may hold values from 0 to 32
- row_index: int32 [1, 512], P(None, 'seq'), may hold values from 0 to 44
- column_index: int32 [1, 512], P(None, 'seq'), may hold values from 0 to 79
- txt_len: int32 [1], replicated, may hold values from 64 to 256
- residual: bfloat16 [1, 512, 3072], P(None, ('seq', 'tp')), may hold values from -6 to 6
- w_proj: bfloat16 [2048, 3072], P('tp'), may hold values from -0.125 to 0.125
- proj_bias: float32 [3072], replicated, may hold values from -3 to 3
- gate: float32 [3072], replicated, may hold values from -4 to 4
Outputs:
- img_out: bfloat16 [1, 512, 3072], P(None, ('seq', 'tp'))
- txt_out: bfloat16 [1, 256, 2048], P(None, None, 'tp')
All inputs are finite; a program needn't handle non-finite values.
Results may differ from a plain program's by a relative error of at most 0.0082.
Values may be sent and summed in bfloat16 or wider, within the bound.
A program may use at most 64 MiB of HBM per device.

v0:
```python
import math
import jax
import jax.numpy as jnp
from jax import lax
from jax.sharding import PartitionSpec as P

HD = 128
rope_base = 256.0
neg_large = -1e30


def rope_tables(frame_index, row_index, column_index, head_dim):
    frame_part = head_dim // 8
    second = (head_dim - frame_part) // 2
    pieces = []
    for places, part_width in (
        (frame_index, frame_part),
        (row_index, second),
        (column_index, second),
    ):
        pair_ids = jnp.arange(part_width // 2).astype(jnp.float32)
        pair_rates = rope_base ** (-2.0 * pair_ids / part_width)
        pieces.append(places.astype(jnp.float32)[:, None] * pair_rates[None, :])
    angles = jnp.repeat(jnp.concatenate(pieces, axis=1), 2, axis=1)
    parity = jnp.arange(head_dim) % 2
    signed = jnp.where(parity == 0, -1.0, 1.0).astype(jnp.float32)
    return (jnp.cos(angles), jnp.sin(angles) * signed[None, :])


def rotate(block_in, cosine, sine_table):
    values = block_in.astype(jnp.float32)
    parity = jnp.arange(values.shape[-1]) % 2
    partner = jnp.where(parity == 0, jnp.roll(values, -1, axis=-1), jnp.roll(values, 1, axis=-1))
    return (values * cosine[:, None, :] + partner * sine_table[:, None, :]).astype(jnp.bfloat16)


def absorb(carry_state, queries, block_keys, block_values, live_keys, score_scale):
    peak, weight_sum, blended = carry_state
    scores = (
        jnp.einsum("cqd,ckd->cqk", queries, block_keys, preferred_element_type=jnp.float32)
        * score_scale
    )
    if live_keys is not None:
        scores = jnp.where(live_keys[:, None, :], scores, neg_large)
    new_peak = jnp.maximum(peak, jnp.max(scores, axis=2))
    weights = jnp.exp(scores - new_peak[:, :, None])
    if live_keys is not None:
        weights = jnp.where(live_keys[:, None, :], weights, 0.0)
    shrink = jnp.exp(peak - new_peak)
    weight_sum = weight_sum * shrink + jnp.sum(weights, axis=2)
    blended = blended * shrink[:, :, None] + jnp.einsum(
        "cqk,ckd->cqd",
        weights.astype(jnp.bfloat16),
        block_values,
        preferred_element_type=jnp.float32,
    )
    return (new_peak, weight_sum, blended)


def shards(
    img_qkv,
    txt_qkv,
    frame_index,
    row_index,
    column_index,
    txt_len,
    residual,
    w_proj,
    proj_bias,
    gate,
):
    clips = img_qkv.shape[0]
    clip_tok = img_qkv.shape[1]
    head_dim = HD
    heads_tp = img_qkv.shape[3] // head_dim
    seq_count = lax.axis_size("seq")
    tp_count = lax.axis_size("tp")
    groups = seq_count // heads_tp
    per_group = clip_tok // groups
    txt_total = txt_qkv.shape[1]
    txt_share = txt_total // groups
    position = lax.axis_index("seq")
    my_head = position % heads_tp
    my_group = position // heads_tp
    score_scale = 1.0 / math.sqrt(head_dim)
    cosine, sine_table = rope_tables(
        frame_index.reshape(-1), row_index.reshape(-1), column_index.reshape(-1), head_dim
    )
    img_query = rotate(
        img_qkv[:, :, 0].reshape(clips * clip_tok, heads_tp, head_dim), cosine, sine_table
    ).reshape(clips, clip_tok, heads_tp, head_dim)
    img_key = rotate(
        img_qkv[:, :, 1].reshape(clips * clip_tok, heads_tp, head_dim), cosine, sine_table
    ).reshape(clips, clip_tok, heads_tp, head_dim)
    img_value = img_qkv[:, :, 2].reshape(clips, clip_tok, heads_tp, head_dim)
    query_send = (
        img_query.reshape(clips, groups, per_group, heads_tp, head_dim)
        .transpose(1, 3, 0, 2, 4)
        .reshape(seq_count, clips * per_group, head_dim)
    )
    key_value = jnp.stack([img_key, img_value], axis=2)
    txt_head = lax.dynamic_slice_in_dim(txt_qkv, my_head * head_dim, head_dim, 3)
    txt_query = lax.dynamic_slice_in_dim(txt_head[:, :, 0], my_group * txt_share, txt_share, 1)
    img_rows_count = seq_count * per_group
    query_rows = img_rows_count + txt_share
    start_state = (
        jnp.full((clips, query_rows), neg_large, jnp.float32),
        jnp.zeros((clips, query_rows), jnp.float32),
        jnp.zeros((clips, query_rows, head_dim), jnp.float32),
    )
    copies = jnp.broadcast_to(
        key_value.transpose(3, 0, 1, 2, 4)[None], (groups, heads_tp, clips, clip_tok, 2, head_dim)
    ).reshape(seq_count, clips, clip_tok, 2, head_dim)
    query_recv, pair_recv = (
        lax.all_to_all(query_send, "seq", split_axis=0, concat_axis=0, tiled=True),
        lax.all_to_all(copies, "seq", split_axis=0, concat_axis=0, tiled=True),
    )
    ordered = (
        query_recv.reshape(seq_count, clips, per_group, head_dim)
        .transpose(1, 0, 2, 3)
        .reshape(clips, img_rows_count, head_dim)
    )
    queries = jnp.concatenate([ordered, txt_query], axis=1)
    sources = max(1, min(seq_count, 2048 // clip_tok))
    while seq_count % sources:
        sources -= 1
    all_pairs = pair_recv.transpose(1, 0, 2, 3, 4).reshape(
        clips, seq_count // sources, sources * clip_tok, 2, head_dim
    )
    key_blocks = all_pairs.transpose(1, 0, 2, 3, 4)

    def sweep_block(carry_state, key_block):
        return (
            absorb(carry_state, queries, key_block[:, :, 0], key_block[:, :, 1], None, score_scale),
            None,
        )

    carry_state, unused = lax.scan(sweep_block, start_state, key_blocks)
    txt_live = jnp.arange(txt_total)[None, :] < txt_len[:, None]
    peak, weight_sum, blended = absorb(
        carry_state, queries, txt_head[:, :, 1], txt_head[:, :, 2], txt_live, score_scale
    )
    attended = (blended / weight_sum[:, :, None]).astype(jnp.bfloat16)
    img_part = (
        attended[:, :img_rows_count]
        .reshape(clips, seq_count, per_group, head_dim)
        .transpose(1, 0, 2, 3)
    )
    txt_part = attended[:, img_rows_count:]
    returned = lax.all_to_all(img_part, "seq", split_axis=0, concat_axis=0, tiled=True)
    home_rows = (
        returned.reshape(groups, heads_tp, clips, per_group, head_dim)
        .transpose(2, 0, 3, 1, 4)
        .reshape(clips, clip_tok, heads_tp * head_dim)
    )
    txt_index = my_group * txt_share + jnp.arange(txt_share)
    txt_keep = (txt_index[None, :] < txt_len[:, None])[:, :, None]
    txt_part = jnp.where(txt_keep, txt_part, jnp.zeros_like(txt_part))
    gathered = lax.all_gather(txt_part[None], "seq", axis=0, tiled=True)
    txt_out = (
        gathered.reshape(groups, heads_tp, clips, txt_share, head_dim)
        .transpose(2, 0, 3, 1, 4)
        .reshape(clips, txt_total, heads_tp * head_dim)
    )
    row_share = clip_tok // tp_count
    share_rows = clips * row_share
    ordered_rows = (
        home_rows.reshape(clips, tp_count, row_share, heads_tp * head_dim)
        .transpose(1, 0, 2, 3)
        .reshape(tp_count * share_rows, heads_tp * head_dim)
    )
    projected = lax.psum_scatter(
        jnp.dot(ordered_rows, w_proj, preferred_element_type=jnp.float32).astype(jnp.bfloat16),
        "tp",
        scatter_dimension=0,
        tiled=True,
    ).astype(jnp.float32)
    projected = projected.reshape(clips, row_share, projected.shape[1])
    img_out = (
        residual.astype(jnp.float32) + gate[None, None, :] * (projected + proj_bias[None, None, :])
    ).astype(jnp.bfloat16)
    return (img_out, txt_out)


def solution(mesh):
    in_specs = (
        P(None, "seq", None, "tp"),
        P(None, None, None, "tp"),
        P(None, "seq"),
        P(None, "seq"),
        P(None, "seq"),
        P(),
        P(None, ("seq", "tp"), None),
        P("tp", None),
        P(),
        P(),
    )
    out_specs = (P(None, ("seq", "tp"), None), P(None, None, "tp"))
    return jax.shard_map(shards, mesh=mesh, in_specs=in_specs, out_specs=out_specs, check_vma=False)
```

profile of v0, /device:TPU:0, one launch (start us, length us, event | category | flops | bytes accessed | tf_op | source)
XLA Modules:
  0.0 106.6 jit_solution(7230840717838111667)
XLA Ops:
  7.2 0.0 copy-start
  7.2 0.0 copy-start.6
  7.2 0.0 copy-start.4
  7.2 0.0 copy-start.5
  7.3 1.0 convert_bitcast_fusion.1
  8.3 0.1 fusion.35
  8.4 0.1 fusion.34
  8.5 0.0 copy-done.6
  8.6 0.0 copy-done.4
  8.6 0.0 copy-done.5
  8.6 0.1 broadcast_multiply_fusion.4
  8.7 0.1 broadcast_multiply_fusion.3
  8.7 0.1 fusion.26
  8.9 0.1 sin.17
  9.1 0.2 broadcast_multiply_fusion
  9.3 0.1 copy.52
  9.4 0.1 cos.17
  9.5 0.1 copy.45
  9.6 0.2 fusion.24
  9.7 0.6 copy.53
  10.4 8.3 %all-to-all-start = ((bf16[16,16,128]{2,1,0:T(8,128)(2,1)}), bf16[16,16,128]{2,1,0:T(8,128)(2,1)S(1)}, u32[]{:S(2)}, u32[]{:S(2)}) async-start(bf16[16,16,128]{2,1,0:T(8,128)(2,1)} %bitcast.8), calls=%async_computation | async-start | bytes 131072 | tf_op jit(solution)/shard_map/all_to_all | solution.py:115
  18.8 0.1 fusion.36
  18.9 0.1 slice_bitcast_fusion.4
  19.0 0.1 copy.54
  19.0 0.1 broadcast_multiply_fusion.1
  19.1 0.1 copy.59
  19.2 0.1 copy.57
  19.3 0.1 copy.55
  19.5 0.2 copy.56
  19.6 0.1 copy.58
  19.8 0.1 fusion.21
  20.0 6.2 %all-to-all-done = bf16[16,16,128]{2,1,0:T(8,128)(2,1)S(1)} async-done(((bf16[16,16,128]{2,1,0:T(8,128)(2,1)}), bf16[16,16,128]{2,1,0:T(8,128)(2,1)S(1)}, u32[]{:S(2)}, u32[]{:S(2)}) %all-to-all-start) | async-done | bytes 65568 | tf_op jit(solution)/shard_map/all_to_all | solution.py:115
  26.3 0.8 broadcast_in_dim.105
  27.0 3.5 %all-to-all-start.1 = ((bf16[16,1,32,2,128]{4,2,3,1,0:T(8,128)(2,1)}), bf16[16,1,32,2,128]{4,2,3,1,0:T(8,128)(2,1)S(1)}, u32[]{:S(2)}, u32[]{:S(2)}) async-start(bf16[16,1,32,2,128]{4,2,3,1,0:T(8,128)(2,1)} %bitcast.21), calls=%async_computation.1 | async-start | bytes 524288 | tf_op jit(solution)/shard_map/all_to_all | solution.py:116
  31.2 0.0 copy-done
  31.3 0.2 fusion.38
  31.5 7.5 %all-to-all-done.1 = bf16[16,1,32,2,128]{4,2,3,1,0:T(8,128)(2,1)S(1)} async-done(((bf16[16,1,32,2,128]{4,2,3,1,0:T(8,128)(2,1)}), bf16[16,1,32,2,128]{4,2,3,1,0:T(8,128)(2,1)S(1)}, u32[]{:S(2)}, u32[]{:S(2)}) %all-to-all-start.1) | async-done | bytes 262176 | tf_op jit(solution)/shard_map/all_to_all | solution.py:116
  39.1 0.3 fusion.37
  39.4 0.1 fusion.9
  39.5 0.3 fusion.5
  39.8 0.3 fusion.2
  40.2 0.3 fusion.4
  40.5 0.6 slice.88
  41.2 3.7 %all-to-all-start.2 = ((bf16[16,1,16,128]{3,2,1,0:T(8,128)(2,1)}), bf16[16,1,16,128]{3,2,1,0:T(8,128)(2,1)S(1)}, u32[]{:S(2)}, u32[]{:S(2)}) async-start(bf16[16,1,16,128]{3,2,1,0:T(8,128)(2,1)} %bitcast.30), calls=%async_computation.2 | async-start | bytes 131072 | tf_op jit(solution)/shard_map/all_to_all | solution.py:150
  44.9 0.0 reduce-scatter.2.cloned.1.call-start
  44.9 7.5 %all-to-all-done.2 = bf16[16,1,16,128]{3,2,1,0:T(8,128)(2,1)S(1)} async-done(((bf16[16,1,16,128]{3,2,1,0:T(8,128)(2,1)}), bf16[16,1,16,128]{3,2,1,0:T(8,128)(2,1)S(1)}, u32[]{:S(2)}, u32[]{:S(2)}) %all-to-all-start.2) | async-done | bytes 65568 | tf_op jit(solution)/shard_map/all_to_all | solution.py:150
  52.4 4.7 %convolution_convert_fusion = bf16[32,3072]{1,0:T(8,128)(2,1)} fusion(bf16[1024,3072]{1,0:T(8,128)(2,1)} %param.17, bf16[4,8,8,128]{3,2,1,0:T(8,128)(2,1)S(1)} %bitcast.138), kind=kOutput, calls=%fused_computation | convolution fusion | flops 201424896 | bytes 6553600 | tf_op jit(solution)/shard_map/dot_general | solution.py:173
  57.1 0.0 copy-start.1
  57.1 0.0 copy-start.2
  57.1 0.0 copy-start.3
  57.1 0.0 reduce-scatter.2.cloned.1.call-update
  57.1 0.1 slice_select_fusion
  57.2 39.6 %all-gather = bf16[16,128,128]{2,1,0:T(8,128)(2,1)S(1)} all-gather(bf16[1,128,128]{2,1,0:T(8,128)(2,1)S(1)} %slice_select_fusion), channel_id=2, replica_groups=mesh['seq'=16,'tp'=2] {'seq'}, dimensions={0}, use_global_device_ids=true | all-gather | bytes 557056 | tf_op jit(solution)/shard_map/all_gather | solution.py:159
  96.8 0.3 copy.65
  97.1 1.0 reshape.419
  98.1 0.0 reduce-scatter.2.cloned.1.call-done
  98.1 0.0 copy-done.1
  98.1 0.0 copy-done.2
  98.1 0.0 copy-done.3
  98.1 1.6 %fusion.12 = bf16[1,16,3072]{2,1,0:T(8,128)(2,1)} fusion(bf16[16,3072]{1,0:T(8,128)(2,1)} %reduce-scatter.2.cloned.1.call-done, bf16[1,16,3072]{2,1,0:T(8,128)(2,1)S(1)} %copy-done.1, f32[3072]{0:T(1024)S(1)} %copy-done.2, f32[3072]{0:T(1024)S(1)} %copy-done.3), kind=kLoop, calls=%fused_computation.18 | loop fusion | flops 294912 | bytes 319488 | tf_op jit(solution)/shard_map/convert_element_type | solution.py:181
  (20 shorter events, 0.3 us)
Async XLA Ops:
  7.2 24.1 %copy-start = (bf16[1,256,3,1024]{3,1,2,0:T(8,128)(2,1)S(1)}, bf16[1,256,3,1024]{3,1,2,0:T(8,128)(2,1)}, u32[]{:S(2)}) copy-start(bf16[1,256,3,1024]{3,1,2,0:T(8,128)(2,1)} %param.11) | copy-start | bytes 4718596
  7.2 1.4 %copy-start.6 = (s32[1,32]{1,0:T(1,128)S(1)}, s32[1,32]{1,0:T(1,128)}, u32[]{:S(2)}) copy-start(s32[1,32]{1,0:T(1,128)} %param.12) | copy-start | bytes 388
  7.2 1.4 %copy-start.4 = (s32[1,32]{1,0:T(1,128)S(1)}, s32[1,32]{1,0:T(1,128)}, u32[]{:S(2)}) copy-start(s32[1,32]{1,0:T(1,128)} %param.14) | copy-start | bytes 388
  7.2 1.4 %copy-start.5 = (s32[1,32]{1,0:T(1,128)S(1)}, s32[1,32]{1,0:T(1,128)}, u32[]{:S(2)}) copy-start(s32[1,32]{1,0:T(1,128)} %param.13) | copy-start | bytes 388
  10.4 15.9 %all-to-all-start = ((bf16[16,16,128]{2,1,0:T(8,128)(2,1)}), bf16[16,16,128]{2,1,0:T(8,128)(2,1)S(1)}, u32[]{:S(2)}, u32[]{:S(2)}) async-start(bf16[16,16,128]{2,1,0:T(8,128)(2,1)} %bitcast.8), calls=%async_computation | async-start | bytes 131072 | tf_op jit(solution)/shard_map/all_to_all | solution.py:115
  27.0 12.0 %all-to-all-start.1 = ((bf16[16,1,32,2,128]{4,2,3,1,0:T(8,128)(2,1)}), bf16[16,1,32,2,128]{4,2,3,1,0:T(8,128)(2,1)S(1)}, u32[]{:S(2)}, u32[]{:S(2)}) async-start(bf16[16,1,32,2,128]{4,2,3,1,0:T(8,128)(2,1)} %bitcast.21), calls=%async_computation.1 | async-start | bytes 524288 | tf_op jit(solution)/shard_map/all_to_all | solution.py:116
  41.2 11.2 %all-to-all-start.2 = ((bf16[16,1,16,128]{3,2,1,0:T(8,128)(2,1)}), bf16[16,1,16,128]{3,2,1,0:T(8,128)(2,1)S(1)}, u32[]{:S(2)}, u32[]{:S(2)}) async-start(bf16[16,1,16,128]{3,2,1,0:T(8,128)(2,1)} %bitcast.30), calls=%async_computation.2 | async-start | bytes 131072 | tf_op jit(solution)/shard_map/all_to_all | solution.py:150
  44.9 53.3 %reduce-scatter.2.cloned.1.call-start = ((), (), s32[]{:S(2)}) async-start(), calls=%async_computation.4 | async-start | bytes 294912 | tf_op jit(solution)/shard_map/reduce_scatter | solution.py:172
  57.1 41.0 %copy-start.1 = (bf16[1,16,3072]{2,1,0:T(8,128)(2,1)S(1)}, bf16[1,16,3072]{2,1,0:T(8,128)(2,1)}, u32[]{:S(2)}) copy-start(bf16[1,16,3072]{2,1,0:T(8,128)(2,1)} %param.16) | copy-start | bytes 294916
  57.1 41.0 %copy-start.2 = (f32[3072]{0:T(1024)S(1)}, f32[3072]{0:T(1024)}, u32[]{:S(2)}) copy-start(f32[3072]{0:T(1024)} %param.18) | copy-start | bytes 36868
  57.1 41.0 %copy-start.3 = (f32[3072]{0:T(1024)S(1)}, f32[3072]{0:T(1024)}, u32[]{:S(2)}) copy-start(f32[3072]{0:T(1024)} %param.19) | copy-start | bytes 36868
Sparse Core Ops, SparseCore 0:
  57.2 4.3 reduce-scatter.1
where the time goes:
time: 107 us
  blocking collectives  39.6 us (37%)
  waiting for transfers between devices  21.2 us (20%)
  starting transfers between devices  15.6 us (15%)
  between operations  15 us (14%)
  matrix products  5.93 us (6%)
  local copies, waits for them, and re-layouts  5.11 us (5%)
  other arithmetic  4.09 us (4%)
    all_gather x1, blocking collectives, shards(): gathered = lax.all_gather(txt_part[None], 'seq', axis=0, tiled=True)  39.6 us
    all_to_all x1, starting transfers between devices, shards(): lax.all_to_all(query_send, 'seq', split_axis=0, concat_axis=0, tiled=True)  8.34 us
    all_to_all x1, waiting for transfers between devices, shards(): lax.all_to_all(copies, 'seq', split_axis=0, concat_axis=0, tiled=True)  7.49 us
    all_to_all x1, waiting for transfers between devices, shards(): lax.all_to_all(img_part, 'seq', split_axis=0, concat_axis=0, tiled=True)  7.47 us
    all_to_all x1, waiting for transfers between devices, shards(): lax.all_to_all(query_send, 'seq', split_axis=0, concat_axis=0, tiled=True)  6.25 us
    dot_general x1, matrix products, shards(): jnp.dot(ordered_rows, w_proj, preferred_element_type=jnp.float32)  4.66 us
    all_to_all x1, starting transfers between devices, shards(): lax.all_to_all(img_part, 'seq', split_axis=0, concat_axis=0, tiled=True)  3.69 us
    all_to_all x1, starting transfers between devices, shards(): lax.all_to_all(copies, 'seq', split_axis=0, concat_axis=0, tiled=True)  3.53 us
  transfers between devices with their start and end apart: 4, of which 3 were waited for; matrix products, arithmetic and copies ran while one was open for 3% of the time, Pallas kernels for 0%

commit v1 on v0

--- a/solution.py
+++ b/solution.py
@@ -156,7 +156,12 @@
     txt_index = my_group * txt_share + jnp.arange(txt_share)
     txt_keep = (txt_index[None, :] < txt_len[:, None])[:, :, None]
     txt_part = jnp.where(txt_keep, txt_part, jnp.zeros_like(txt_part))
-    gathered = lax.all_gather(txt_part[None], "seq", axis=0, tiled=True)
+    ring = [txt_part[None]]
+    for hop in range(15):
+        ring.append(lax.ppermute(ring[-1], "seq", [(dev, (dev + 1) % 16) for dev in range(16)]))
+    gathered = jnp.roll(
+        jnp.concatenate(ring[::-1], axis=0), (lax.axis_index("seq") + 1) * ring[0].shape[0], axis=0
+    )
     txt_out = (
         gathered.reshape(groups, heads_tp, clips, txt_share, head_dim)
         .transpose(2, 0, 3, 1, 4)

time: 107 us -> 170 us (1.59)
  waiting for transfers between devices: 21.2 us -> 116 us
  blocking collectives: 39.6 us -> 0 us
  starting transfers between devices: 15.6 us -> 22.4 us
    ppermute x0 -> x15, waiting for transfers between devices: none -> 98 us  [shards(): lax.ppermute(ring[-1], 'seq', [(dev, (dev + 1) % 16) for dev in range(16)])]
    all_gather x1 -> x0, blocking collectives: 39.6 us -> none  [shards(): gathered = lax.all_gather(txt_part[None], 'seq', axis=0, tiled=True)]
    all_to_all x1, waiting for transfers between devices: 7.47 us -> 0.01 us  [shards(): lax.all_to_all(img_part, 'seq', split_axis=0, concat_axis=0, tiled=True)]
    reduce_scatter x1, waiting for transfers between devices: 0.01 us -> 4.28 us  [shards(): lax.psum_scatter(jnp.dot(ordered_rows, w_proj, preferred_element_type=jnp...]
    ppermute x0 -> x15, starting transfers between devices: none -> 3.5 us  [shards(): lax.ppermute(ring[-1], 'seq', [(dev, (dev + 1) % 16) for dev in range(16)])]
    all_to_all x1, starting transfers between devices: 3.69 us -> 7 us  [shards(): lax.all_to_all(img_part, 'seq', split_axis=0, concat_axis=0, tiled=True)]
  transfers between devices with their start and end apart: 4 -> 19, of which waited for: 3 -> 17; matrix products, arithmetic and copies ran while one was open for 3% -> 5% of each run, Pallas kernels for 0% -> 0%
where the time goes in v1:
time: 170 us; the launch traced here: 169 us
  waiting for transfers between devices  116 us (68%)
  starting transfers between devices  22.4 us (13%)
  between operations  15.3 us (9%)
  matrix products  5.94 us (3%)
  local copies, waits for them, and re-layouts  5.49 us (3%)
  other arithmetic  4.26 us (3%)
    ppermute x15, waiting for transfers between devices, shards(): lax.ppermute(ring[-1], 'seq', [(dev, (dev + 1) % 16) for dev in range(16)])  98 us
    all_to_all x1, starting transfers between devices, shards(): lax.all_to_all(query_send, 'seq', split_axis=0, concat_axis=0, tiled=True)  8.34 us
    all_to_all x1, waiting for transfers between devices, shards(): lax.all_to_all(copies, 'seq', split_axis=0, concat_axis=0, tiled=True)  8.13 us
    all_to_all x1, starting transfers between devices, shards(): lax.all_to_all(img_part, 'seq', split_axis=0, concat_axis=0, tiled=True)  7 us
    all_to_all x1, waiting for transfers between devices, shards(): lax.all_to_all(query_send, 'seq', split_axis=0, concat_axis=0, tiled=True)  5.6 us
    dot_general x1, matrix products, shards(): jnp.dot(ordered_rows, w_proj, preferred_element_type=jnp.float32)  4.67 us
    reduce_scatter x1, waiting for transfers between devices, shards(): lax.psum_scatter(jnp.dot(ordered_rows, w_proj, preferred_element_type=jnp...  4.28 us
    all_to_all x1, starting transfers between devices, shards(): lax.all_to_all(copies, 'seq', split_axis=0, concat_axis=0, tiled=True)  3.53 us
  transfers between devices with their start and end apart: 19, of which 17 were waited for; matrix products, arithmetic and copies ran while one was open for 5% of the time, Pallas kernels for 0%

profile of v1, /device:TPU:0, one launch (start us, length us, event | category | flops | bytes accessed | tf_op | source)
XLA Modules:
  0.0 169.4 jit_solution(9270939822013858922)
XLA Ops:
  7.2 0.0 copy-start
  7.2 1.0 convert_bitcast_fusion.1
  8.3 0.1 fusion.36
  8.4 0.1 fusion.35
  8.6 0.1 broadcast_multiply_fusion.4
  8.7 0.1 broadcast_multiply_fusion.3
  8.7 0.1 fusion.27
  8.9 0.1 sin.17
  9.1 0.2 broadcast_multiply_fusion
  9.3 0.1 copy.50
  9.4 0.1 cos.17
  9.5 0.1 copy.43
  9.6 0.2 fusion.24
  9.7 0.6 copy.51
  10.4 8.3 %all-to-all-start = ((bf16[16,16,128]{2,1,0:T(8,128)(2,1)}), bf16[16,16,128]{2,1,0:T(8,128)(2,1)S(1)}, u32[]{:S(2)}, u32[]{:S(2)}) async-start(bf16[16,16,128]{2,1,0:T(8,128)(2,1)} %bitcast.8), calls=%async_computation | async-start | bytes 131072 | tf_op jit(solution)/shard_map/all_to_all | solution.py:115
  18.8 0.1 fusion.37
  18.9 0.1 slice_bitcast_fusion.4
  19.0 0.1 broadcast_multiply_fusion.1
  19.1 0.1 copy.57
  19.1 0.1 copy.52
  19.2 0.1 copy.53
  19.3 0.2 copy.54
  19.5 0.1 copy.55
  19.6 0.1 copy.56
  19.8 0.1 fusion.21
  20.7 5.6 %all-to-all-done = bf16[16,16,128]{2,1,0:T(8,128)(2,1)S(1)} async-done(((bf16[16,16,128]{2,1,0:T(8,128)(2,1)}), bf16[16,16,128]{2,1,0:T(8,128)(2,1)S(1)}, u32[]{:S(2)}, u32[]{:S(2)}) %all-to-all-start) | async-done | bytes 65568 | tf_op jit(solution)/shard_map/all_to_all | solution.py:115
  26.3 0.8 broadcast_in_dim.105
  27.0 3.5 %all-to-all-start.1 = ((bf16[16,1,32,2,128]{4,2,3,1,0:T(8,128)(2,1)}), bf16[16,1,32,2,128]{4,2,3,1,0:T(8,128)(2,1)S(1)}, u32[]{:S(2)}, u32[]{:S(2)}) async-start(bf16[16,1,32,2,128]{4,2,3,1,0:T(8,128)(2,1)} %bitcast.21), calls=%async_computation.1 | async-start | bytes 524288 | tf_op jit(solution)/shard_map/all_to_all | solution.py:116
  30.7 0.2 fusion.39
  30.9 8.1 %all-to-all-done.1 = bf16[16,1,32,2,128]{4,2,3,1,0:T(8,128)(2,1)S(1)} async-done(((bf16[16,1,32,2,128]{4,2,3,1,0:T(8,128)(2,1)}), bf16[16,1,32,2,128]{4,2,3,1,0:T(8,128)(2,1)S(1)}, u32[]{:S(2)}, u32[]{:S(2)}) %all-to-all-start.1) | async-done | bytes 262176 | tf_op jit(solution)/shard_map/all_to_all | solution.py:116
  39.1 0.3 fusion.38
  39.4 0.3 fusion.5
  39.7 0.1 fusion.9
  39.8 0.3 fusion.2
  40.2 0.3 fusion.4
  40.5 0.1 fusion.25
  40.6 1.5 collective-permute-start
  42.1 6.1 %collective-permute-done = bf16[1,1,128,128]{3,2,1,0:T(8,128)(2,1)S(1)} collective-permute-done((bf16[1,1,128,128]{3,2,1,0:T(8,128)(2,1)S(1)}, bf16[1,1,128,128]{3,2,1,0:T(8,128)(2,1)S(1)}, u32[]{:S(2)}, u32[]{:S(2)}) %collective-permute-start) | collective-permute-done | bytes 32800 | tf_op jit(solution)/shard_map/ppermute | solution.py:161
  48.2 7.5 %collective-permute-done.1 = bf16[1,1,128,128]{3,2,1,0:T(8,128)(2,1)S(1)} collective-permute-done((bf16[1,1,128,128]{3,2,1,0:T(8,128)(2,1)S(1)}, bf16[1,1,128,128]{3,2,1,0:T(8,128)(2,1)S(1)}, u32[]{:S(2)}, u32[]{:S(2)}) %collective-permute-start.1) | collective-permute-done | bytes 32800 | tf_op jit(solution)/shard_map/ppermute | solution.py:161
  55.7 7.5 %collective-permute-done.2 = bf16[1,1,128,128]{3,2,1,0:T(8,128)(2,1)S(1)} collective-permute-done((bf16[1,1,128,128]{3,2,1,0:T(8,128)(2,1)S(1)}, bf16[1,1,128,128]{3,2,1,0:T(8,128)(2,1)S(1)}, u32[]{:S(2)}, u32[]{:S(2)}) %collective-permute-start.2) | collective-permute-done | bytes 32800 | tf_op jit(solution)/shard_map/ppermute | solution.py:161
  63.2 7.5 %collective-permute-done.3 = bf16[1,1,128,128]{3,2,1,0:T(8,128)(2,1)S(1)} collective-permute-done((bf16[1,1,128,128]{3,2,1,0:T(8,128)(2,1)S(1)}, bf16[1,1,128,128]{3,2,1,0:T(8,128)(2,1)S(1)}, u32[]{:S(2)}, u32[]{:S(2)}) %collective-permute-start.3) | collective-permute-done | bytes 32800 | tf_op jit(solution)/shard_map/ppermute | solution.py:161
  70.7 7.5 %collective-permute-done.4 = bf16[1,1,128,128]{3,2,1,0:T(8,128)(2,1)S(1)} collective-permute-done((bf16[1,1,128,128]{3,2,1,0:T(8,128)(2,1)S(1)}, bf16[1,1,128,128]{3,2,1,0:T(8,128)(2,1)S(1)}, u32[]{:S(2)}, u32[]{:S(2)}) %collective-permute-start.4) | collective-permute-done | bytes 32800 | tf_op jit(solution)/shard_map/ppermute | solution.py:161
  78.2 7.5 %collective-permute-done.5 = bf16[1,1,128,128]{3,2,1,0:T(8,128)(2,1)S(1)} collective-permute-done((bf16[1,1,128,128]{3,2,1,0:T(8,128)(2,1)S(1)}, bf16[1,1,128,128]{3,2,1,0:T(8,128)(2,1)S(1)}, u32[]{:S(2)}, u32[]{:S(2)}) %collective-permute-start.5) | collective-permute-done | bytes 32800 | tf_op jit(solution)/shard_map/ppermute | solution.py:161
  85.8 7.5 %collective-permute-done.6 = bf16[1,1,128,128]{3,2,1,0:T(8,128)(2,1)S(1)} collective-permute-done((bf16[1,1,128,128]{3,2,1,0:T(8,128)(2,1)S(1)}, bf16[1,1,128,128]{3,2,1,0:T(8,128)(2,1)S(1)}, u32[]{:S(2)}, u32[]{:S(2)}) %collective-permute-start.6) | collective-permute-done | bytes 32800 | tf_op jit(solution)/shard_map/ppermute | solution.py:161
  93.3 7.5 %collective-permute-done.7 = bf16[1,1,128,128]{3,2,1,0:T(8,128)(2,1)S(1)} collective-permute-done((bf16[1,1,128,128]{3,2,1,0:T(8,128)(2,1)S(1)}, bf16[1,1,128,128]{3,2,1,0:T(8,128)(2,1)S(1)}, u32[]{:S(2)}, u32[]{:S(2)}) %collective-permute-start.7) | collective-permute-done | bytes 32800 | tf_op jit(solution)/shard_map/ppermute | solution.py:161
  100.8 7.8 %collective-permute-done.8 = bf16[1,1,128,128]{3,2,1,0:T(8,128)(2,1)S(1)} collective-permute-done((bf16[1,1,128,128]{3,2,1,0:T(8,128)(2,1)S(1)}, bf16[1,1,128,128]{3,2,1,0:T(8,128)(2,1)S(1)}, u32[]{:S(2)}, u32[]{:S(2)}) %collective-permute-start.8) | collective-permute-done | bytes 32800 | tf_op jit(solution)/shard_map/ppermute | solution.py:161
  108.6 7.7 %collective-permute-done.9 = bf16[1,1,128,128]{3,2,1,0:T(8,128)(2,1)S(1)} collective-permute-done((bf16[1,1,128,128]{3,2,1,0:T(8,128)(2,1)S(1)}, bf16[1,1,128,128]{3,2,1,0:T(8,128)(2,1)S(1)}, u32[]{:S(2)}, u32[]{:S(2)}) %collective-permute-start.9) | collective-permute-done | bytes 32800 | tf_op jit(solution)/shard_map/ppermute | solution.py:161
  116.3 0.6 slice.88
  116.9 7.0 %all-to-all-start.2 = ((bf16[16,1,16,128]{3,2,1,0:T(8,128)(2,1)}), bf16[16,1,16,128]{3,2,1,0:T(8,128)(2,1)S(1)}, u32[]{:S(2)}, u32[]{:S(2)}) async-start(bf16[16,1,16,128]{3,2,1,0:T(8,128)(2,1)} %bitcast.30), calls=%async_computation.2 | async-start | bytes 131072 | tf_op jit(solution)/shard_map/all_to_all | solution.py:150
  123.9 0.0 reduce-scatter.2.cloned.1.call-start
  124.0 2.0 %collective-permute-start.11 = (bf16[1,1,128,128]{3,2,1,0:T(8,128)(2,1)S(1)}, bf16[1,1,128,128]{3,2,1,0:T(8,128)(2,1)S(1)}, u32[]{:S(2)}, u32[]{:S(2)}) collective-permute-start(bf16[1,1,128,128]{3,2,1,0:T(8,128)(2,1)S(1)} %collective-permute-done.10), channel_id=1, source_target_pairs={{0,2},{2,4},{4,6},{6,8},{8,10},{10,12},{12,14},{14,16},{16,18},{18... | collective-permute-start | bytes 98312 | tf_op jit(solution)/shard_map/ppermute | solution.py:161
  125.9 6.1 %collective-permute-done.11 = bf16[1,1,128,128]{3,2,1,0:T(8,128)(2,1)S(1)} collective-permute-done((bf16[1,1,128,128]{3,2,1,0:T(8,128)(2,1)S(1)}, bf16[1,1,128,128]{3,2,1,0:T(8,128)(2,1)S(1)}, u32[]{:S(2)}, u32[]{:S(2)}) %collective-permute-start.11) | collective-permute-done | bytes 32800 | tf_op jit(solution)/shard_map/ppermute | solution.py:161
  132.1 7.5 %collective-permute-done.12 = bf16[1,1,128,128]{3,2,1,0:T(8,128)(2,1)S(1)} collective-permute-done((bf16[1,1,128,128]{3,2,1,0:T(8,128)(2,1)S(1)}, bf16[1,1,128,128]{3,2,1,0:T(8,128)(2,1)S(1)}, u32[]{:S(2)}, u32[]{:S(2)}) %collective-permute-start.12) | collective-permute-done | bytes 32800 | tf_op jit(solution)/shard_map/ppermute | solution.py:161
  139.6 7.5 %collective-permute-done.13 = bf16[1,1,128,128]{3,2,1,0:T(8,128)(2,1)S(1)} collective-permute-done((bf16[1,1,128,128]{3,2,1,0:T(8,128)(2,1)S(1)}, bf16[1,1,128,128]{3,2,1,0:T(8,128)(2,1)S(1)}, u32[]{:S(2)}, u32[]{:S(2)}) %collective-permute-start.13) | collective-permute-done | bytes 32800 | tf_op jit(solution)/shard_map/ppermute | solution.py:161
  147.1 4.7 %convolution_convert_fusion = bf16[32,3072]{1,0:T(8,128)(2,1)} fusion(bf16[1024,3072]{1,0:T(8,128)(2,1)} %param.17, bf16[4,8,8,128]{3,2,1,0:T(8,128)(2,1)S(1)} %bitcast.144), kind=kOutput, calls=%fused_computation | convolution fusion | flops 201424896 | bytes 6553600 | tf_op jit(solution)/shard_map/dot_general | solution.py:178
  151.8 0.0 reduce-scatter.2.cloned.1.call-update
  151.8 2.8 %collective-permute-done.14 = bf16[1,1,128,128]{3,2,1,0:T(8,128)(2,1)S(1)} collective-permute-done((bf16[1,1,128,128]{3,2,1,0:T(8,128)(2,1)S(1)}, bf16[1,1,128,128]{3,2,1,0:T(8,128)(2,1)S(1)}, u32[]{:S(2)}, u32[]{:S(2)}) %collective-permute-start.14) | collective-permute-done | bytes 32800 | tf_op jit(solution)/shard_map/ppermute | solution.py:161
  154.8 0.1 constant_dynamic-update-slice_fusion.16
  155.1 0.1 constant_dynamic-update-slice_fusion
  155.2 0.0 copy-start.1
  155.3 0.3 copy.63
  155.7 1.0 reshape.419
  156.7 4.3 %reduce-scatter.2.cloned.1.call-done = bf16[16,3072]{1,0:T(8,128)(2,1)} async-done(((bf16[32,3072]{1,0:T(8,128)(2,1)}), bf16[16,3072]{1,0:T(8,128)(2,1)}) %reduce-scatter.2.cloned.1.call-update) | async-done | bytes 98320 | tf_op jit(solution)/shard_map/reduce_scatter | solution.py:177
  161.0 1.6 fusion.12
  (78 shorter events, 0.7 us)
Async XLA Ops:
  7.2 23.5 %copy-start = (bf16[1,256,3,1024]{3,1,2,0:T(8,128)(2,1)S(1)}, bf16[1,256,3,1024]{3,1,2,0:T(8,128)(2,1)}, u32[]{:S(2)}) copy-start(bf16[1,256,3,1024]{3,1,2,0:T(8,128)(2,1)} %param.11) | copy-start | bytes 4718596
  7.2 1.4 copy-start.6
  7.2 1.4 copy-start.5
  7.2 1.4 copy-start.4
  10.4 15.9 %all-to-all-start = ((bf16[16,16,128]{2,1,0:T(8,128)(2,1)}), bf16[16,16,128]{2,1,0:T(8,128)(2,1)S(1)}, u32[]{:S(2)}, u32[]{:S(2)}) async-start(bf16[16,16,128]{2,1,0:T(8,128)(2,1)} %bitcast.8), calls=%async_computation | async-start | bytes 131072 | tf_op jit(solution)/shard_map/all_to_all | solution.py:115
  27.0 12.0 %all-to-all-start.1 = ((bf16[16,1,32,2,128]{4,2,3,1,0:T(8,128)(2,1)}), bf16[16,1,32,2,128]{4,2,3,1,0:T(8,128)(2,1)S(1)}, u32[]{:S(2)}, u32[]{:S(2)}) async-start(bf16[16,1,32,2,128]{4,2,3,1,0:T(8,128)(2,1)} %bitcast.21), calls=%async_computation.1 | async-start | bytes 524288 | tf_op jit(solution)/shard_map/all_to_all | solution.py:116
  40.6 7.6 %collective-permute-start = (bf16[1,1,128,128]{3,2,1,0:T(8,128)(2,1)S(1)}, bf16[1,1,128,128]{3,2,1,0:T(8,128)(2,1)S(1)}, u32[]{:S(2)}, u32[]{:S(2)}) collective-permute-start(bf16[1,1,128,128]{3,2,1,0:T(8,128)(2,1)S(1)} %fusion.25), channel_id=1, source_target_pairs={{0,2},{2,4},{4,6},{6,8},{8,10},{10,12},{12,14},{14,16},{16,18},{18... | collective-permute-start | bytes 98312 | tf_op jit(solution)/shard_map/ppermute | solution.py:161
  48.2 7.5 %collective-permute-start.1 = (bf16[1,1,128,128]{3,2,1,0:T(8,128)(2,1)S(1)}, bf16[1,1,128,128]{3,2,1,0:T(8,128)(2,1)S(1)}, u32[]{:S(2)}, u32[]{:S(2)}) collective-permute-start(bf16[1,1,128,128]{3,2,1,0:T(8,128)(2,1)S(1)} %collective-permute-done), channel_id=1, source_target_pairs={{0,2},{2,4},{4,6},{6,8},{8,10},{10,12},{12,14},{14,16},{16,18},{18... | collective-permute-start | bytes 98312 | tf_op jit(solution)/shard_map/ppermute | solution.py:161
  55.7 7.5 %collective-permute-start.2 = (bf16[1,1,128,128]{3,2,1,0:T(8,128)(2,1)S(1)}, bf16[1,1,128,128]{3,2,1,0:T(8,128)(2,1)S(1)}, u32[]{:S(2)}, u32[]{:S(2)}) collective-permute-start(bf16[1,1,128,128]{3,2,1,0:T(8,128)(2,1)S(1)} %collective-permute-done.1), channel_id=1, source_target_pairs={{0,2},{2,4},{4,6},{6,8},{8,10},{10,12},{12,14},{14,16},{16,18},{18... | collective-permute-start | bytes 98312 | tf_op jit(solution)/shard_map/ppermute | solution.py:161
  63.2 7.5 %collective-permute-start.3 = (bf16[1,1,128,128]{3,2,1,0:T(8,128)(2,1)S(1)}, bf16[1,1,128,128]{3,2,1,0:T(8,128)(2,1)S(1)}, u32[]{:S(2)}, u32[]{:S(2)}) collective-permute-start(bf16[1,1,128,128]{3,2,1,0:T(8,128)(2,1)S(1)} %collective-permute-done.2), channel_id=1, source_target_pairs={{0,2},{2,4},{4,6},{6,8},{8,10},{10,12},{12,14},{14,16},{16,18},{18... | collective-permute-start | bytes 98312 | tf_op jit(solution)/shard_map/ppermute | solution.py:161
  70.7 7.5 %collective-permute-start.4 = (bf16[1,1,128,128]{3,2,1,0:T(8,128)(2,1)S(1)}, bf16[1,1,128,128]{3,2,1,0:T(8,128)(2,1)S(1)}, u32[]{:S(2)}, u32[]{:S(2)}) collective-permute-start(bf16[1,1,128,128]{3,2,1,0:T(8,128)(2,1)S(1)} %collective-permute-done.3), channel_id=1, source_target_pairs={{0,2},{2,4},{4,6},{6,8},{8,10},{10,12},{12,14},{14,16},{16,18},{18... | collective-permute-start | bytes 98312 | tf_op jit(solution)/shard_map/ppermute | solution.py:161
  78.2 7.5 %collective-permute-start.5 = (bf16[1,1,128,128]{3,2,1,0:T(8,128)(2,1)S(1)}, bf16[1,1,128,128]{3,2,1,0:T(8,128)(2,1)S(1)}, u32[]{:S(2)}, u32[]{:S(2)}) collective-permute-start(bf16[1,1,128,128]{3,2,1,0:T(8,128)(2,1)S(1)} %collective-permute-done.4), channel_id=1, source_target_pairs={{0,2},{2,4},{4,6},{6,8},{8,10},{10,12},{12,14},{14,16},{16,18},{18... | collective-permute-start | bytes 98312 | tf_op jit(solution)/shard_map/ppermute | solution.py:161
  85.7 7.5 %collective-permute-start.6 = (bf16[1,1,128,128]{3,2,1,0:T(8,128)(2,1)S(1)}, bf16[1,1,128,128]{3,2,1,0:T(8,128)(2,1)S(1)}, u32[]{:S(2)}, u32[]{:S(2)}) collective-permute-start(bf16[1,1,128,128]{3,2,1,0:T(8,128)(2,1)S(1)} %collective-permute-done.5), channel_id=1, source_target_pairs={{0,2},{2,4},{4,6},{6,8},{8,10},{10,12},{12,14},{14,16},{16,18},{18... | collective-permute-start | bytes 98312 | tf_op jit(solution)/shard_map/ppermute | solution.py:161
  93.3 7.5 %collective-permute-start.7 = (bf16[1,1,128,128]{3,2,1,0:T(8,128)(2,1)S(1)}, bf16[1,1,128,128]{3,2,1,0:T(8,128)(2,1)S(1)}, u32[]{:S(2)}, u32[]{:S(2)}) collective-permute-start(bf16[1,1,128,128]{3,2,1,0:T(8,128)(2,1)S(1)} %collective-permute-done.6), channel_id=1, source_target_pairs={{0,2},{2,4},{4,6},{6,8},{8,10},{10,12},{12,14},{14,16},{16,18},{18... | collective-permute-start | bytes 98312 | tf_op jit(solution)/shard_map/ppermute | solution.py:161
  100.8 7.8 %collective-permute-start.8 = (bf16[1,1,128,128]{3,2,1,0:T(8,128)(2,1)S(1)}, bf16[1,1,128,128]{3,2,1,0:T(8,128)(2,1)S(1)}, u32[]{:S(2)}, u32[]{:S(2)}) collective-permute-start(bf16[1,1,128,128]{3,2,1,0:T(8,128)(2,1)S(1)} %collective-permute-done.7), channel_id=1, source_target_pairs={{0,2},{2,4},{4,6},{6,8},{8,10},{10,12},{12,14},{14,16},{16,18},{18... | collective-permute-start | bytes 98312 | tf_op jit(solution)/shard_map/ppermute | solution.py:161
  108.6 7.7 %collective-permute-start.9 = (bf16[1,1,128,128]{3,2,1,0:T(8,128)(2,1)S(1)}, bf16[1,1,128,128]{3,2,1,0:T(8,128)(2,1)S(1)}, u32[]{:S(2)}, u32[]{:S(2)}) collective-permute-start(bf16[1,1,128,128]{3,2,1,0:T(8,128)(2,1)S(1)} %collective-permute-done.8), channel_id=1, source_target_pairs={{0,2},{2,4},{4,6},{6,8},{8,10},{10,12},{12,14},{14,16},{16,18},{18... | collective-permute-start | bytes 98312 | tf_op jit(solution)/shard_map/ppermute | solution.py:161
  116.3 7.7 %collective-permute-start.10 = (bf16[1,1,128,128]{3,2,1,0:T(8,128)(2,1)S(1)}, bf16[1,1,128,128]{3,2,1,0:T(8,128)(2,1)S(1)}, u32[]{:S(2)}, u32[]{:S(2)}) collective-permute-start(bf16[1,1,128,128]{3,2,1,0:T(8,128)(2,1)S(1)} %collective-permute-done.9), channel_id=1, source_target_pairs={{0,2},{2,4},{4,6},{6,8},{8,10},{10,12},{12,14},{14,16},{16,18},{18... | collective-permute-start | bytes 98312 | tf_op jit(solution)/shard_map/ppermute | solution.py:161
  116.9 22.7 %all-to-all-start.2 = ((bf16[16,1,16,128]{3,2,1,0:T(8,128)(2,1)}), bf16[16,1,16,128]{3,2,1,0:T(8,128)(2,1)S(1)}, u32[]{:S(2)}, u32[]{:S(2)}) async-start(bf16[16,1,16,128]{3,2,1,0:T(8,128)(2,1)} %bitcast.30), calls=%async_computation.2 | async-start | bytes 131072 | tf_op jit(solution)/shard_map/all_to_all | solution.py:150
  123.9 37.1 %reduce-scatter.2.cloned.1.call-start = ((), (), s32[]{:S(2)}) async-start(), calls=%async_computation.4 | async-start | bytes 294912 | tf_op jit(solution)/shard_map/reduce_scatter | solution.py:177
  124.0 8.1 %collective-permute-start.11 = (bf16[1,1,128,128]{3,2,1,0:T(8,128)(2,1)S(1)}, bf16[1,1,128,128]{3,2,1,0:T(8,128)(2,1)S(1)}, u32[]{:S(2)}, u32[]{:S(2)}) collective-permute-start(bf16[1,1,128,128]{3,2,1,0:T(8,128)(2,1)S(1)} %collective-permute-done.10), channel_id=1, source_target_pairs={{0,2},{2,4},{4,6},{6,8},{8,10},{10,12},{12,14},{14,16},{16,18},{18... | collective-permute-start | bytes 98312 | tf_op jit(solution)/shard_map/ppermute | solution.py:161
  132.1 7.5 %collective-permute-start.12 = (bf16[1,1,128,128]{3,2,1,0:T(8,128)(2,1)S(1)}, bf16[1,1,128,128]{3,2,1,0:T(8,128)(2,1)S(1)}, u32[]{:S(2)}, u32[]{:S(2)}) collective-permute-start(bf16[1,1,128,128]{3,2,1,0:T(8,128)(2,1)S(1)} %collective-permute-done.11), channel_id=1, source_target_pairs={{0,2},{2,4},{4,6},{6,8},{8,10},{10,12},{12,14},{14,16},{16,18},{18... | collective-permute-start | bytes 98312 | tf_op jit(solution)/shard_map/ppermute | solution.py:161
  139.6 7.5 %collective-permute-start.13 = (bf16[1,1,128,128]{3,2,1,0:T(8,128)(2,1)S(1)}, bf16[1,1,128,128]{3,2,1,0:T(8,128)(2,1)S(1)}, u32[]{:S(2)}, u32[]{:S(2)}) collective-permute-start(bf16[1,1,128,128]{3,2,1,0:T(8,128)(2,1)S(1)} %collective-permute-done.12), channel_id=1, source_target_pairs={{0,2},{2,4},{4,6},{6,8},{8,10},{10,12},{12,14},{14,16},{16,18},{18... | collective-permute-start | bytes 98312 | tf_op jit(solution)/shard_map/ppermute | solution.py:161
  147.1 7.5 %collective-permute-start.14 = (bf16[1,1,128,128]{3,2,1,0:T(8,128)(2,1)S(1)}, bf16[1,1,128,128]{3,2,1,0:T(8,128)(2,1)S(1)}, u32[]{:S(2)}, u32[]{:S(2)}) collective-permute-start(bf16[1,1,128,128]{3,2,1,0:T(8,128)(2,1)S(1)} %collective-permute-done.13), channel_id=1, source_target_pairs={{0,2},{2,4},{4,6},{6,8},{8,10},{10,12},{12,14},{14,16},{16,18},{18... | collective-permute-start | bytes 98312 | tf_op jit(solution)/shard_map/ppermute | solution.py:161
  155.2 5.7 %copy-start.1 = (bf16[1,16,3072]{2,1,0:T(8,128)(2,1)S(1)}, bf16[1,16,3072]{2,1,0:T(8,128)(2,1)}, u32[]{:S(2)}) copy-start(bf16[1,16,3072]{2,1,0:T(8,128)(2,1)} %param.16) | copy-start | bytes 294916
  155.2 5.7 %copy-start.2 = (f32[3072]{0:T(1024)S(1)}, f32[3072]{0:T(1024)}, u32[]{:S(2)}) copy-start(f32[3072]{0:T(1024)} %param.18) | copy-start | bytes 36868
  155.3 5.7 %copy-start.3 = (f32[3072]{0:T(1024)S(1)}, f32[3072]{0:T(1024)}, u32[]{:S(2)}) copy-start(f32[3072]{0:T(1024)} %param.19) | copy-start | bytes 36868
Sparse Core Ops, SparseCore 0:
  151.9 9.0 reduce-scatter.1
